TPU v7x, 256 devices: a whole 4x4x8 slice. The times are simulated.
256 devices in a mesh: section: 8 (over y, core), expert: 32 (over z, x).
Axes of the slice: x: 4, y: 4, z: 8, core: 2. Of those that a mesh axis runs over, the one named last changes fastest.
Arguments:
- tokens: bfloat16 [2, 4096, 2048], P(None, 'expert'), may hold values from -6 to 6
- norm_gain: float32 [8, 2048], P('section'), may hold values from 0.1 to 1.9
- w_gate: bfloat16 [8, 32, 2048, 704], P('section', 'expert'), may hold values from -0.125 to 0.125
- w_up: bfloat16 [8, 32, 2048, 704], P('section', 'expert'), may hold values from -0.125 to 0.125
- w_down: bfloat16 [8, 32, 704, 2048], P('section', 'expert'), may hold values from -0.21875 to 0.21875
- expert_ids: int32 [8, 2, 4096, 6], P('section', None, 'expert'), may hold values from 0 to 31, all different within a row; in each aligned block of 128 rows (0 to 127, 128 to 255, ..., all dimensions but the last counted through in order) at most 25 rows name the same one
- route_weight: float32 [8, 2, 4096, 6], P('section', None, 'expert'), may hold values from 0.1 to 1
Outputs:
- stream: bfloat16 [8, 2, 4096, 2048], P('section', None, 'expert')
Inputs may be any that keep to these rules, and one draw needn't show every extreme that they name: `expert_ids`: A token names 6 different experts. In each aligned block of 128 tokens (the tokens of one device in one layer and micro-batch) no expert is named by more than 25 tokens, a bound that some block reaches.
All inputs are finite; a program needn't handle non-finite values.
Results may differ from a plain program's by a relative error of at most 0.025.
Values may be sent and summed in bfloat16 or wider, within the bound.
A program may use at most 128 MiB of HBM per device.

v0:
```python
import jax
import jax.numpy as jnp
from jax import lax
from jax.sharding import PartitionSpec as P

epsilon = 1e-06


def passed_along(block, axis, distance):
    devices = range(lax.axis_size(axis))
    route = [(i - distance, i) for i in devices if i - distance in devices]
    return lax.ppermute(block, axis, route)


def rms_normed(row_block, norm_scale):
    values = row_block.astype(jnp.float32)
    inverse_rms = lax.rsqrt(jnp.mean(values * values, axis=-1, keepdims=True) + epsilon)
    return (values * inverse_rms * norm_scale).astype(jnp.bfloat16)


def swiglu(inputs, gate_matrix, up_matrix, down_matrix):
    gate_proj = jnp.dot(inputs, gate_matrix, preferred_element_type=jnp.float32)
    upward = jnp.dot(inputs, up_matrix, preferred_element_type=jnp.float32)
    hidden = (jax.nn.silu(gate_proj) * upward).astype(jnp.bfloat16)
    return jnp.dot(hidden, down_matrix, preferred_element_type=jnp.float32).astype(jnp.bfloat16)


def per_device(tokens, norm_gain, w_gate, w_up, w_down, expert_ids, route_weight):
    groups = lax.axis_size("expert")
    sections = lax.axis_size("section")
    position = lax.axis_index("section")
    micro_count, tok_rows, model_width = tokens.shape
    fanout = expert_ids.shape[-1]
    capacity = tok_rows * fanout // groups + 1
    norm_scale = norm_gain[0]
    gate_matrix = w_gate[0, 0]
    up_matrix = w_up[0, 0]
    down_matrix = w_down[0, 0]

    def layer_step(residual, route_ids, weights, active):
        flat_ids = route_ids.reshape(-1)
        onehot = (flat_ids[:, None] == jnp.arange(groups, dtype=jnp.int32)[None, :]).astype(
            jnp.int32
        )
        slot_index = jnp.sum((jnp.cumsum(onehot, axis=0) - 1) * onehot, axis=1)
        target = flat_ids * capacity + slot_index

        def build(residual_in):
            slot_rows = jnp.arange(groups * capacity, dtype=jnp.int32)[:, None, None]
            selector = (
                (target.reshape(tok_rows, fanout)[None, :, :] == slot_rows)
                .any(axis=2)
                .astype(jnp.bfloat16)
            )
            return jnp.dot(selector, residual_in, preferred_element_type=jnp.float32).astype(
                jnp.bfloat16
            )

        def skip_build(residual_in):
            return jnp.zeros((groups * capacity, model_width), jnp.bfloat16)

        outgoing = lax.cond(active, build, skip_build, residual)
        outgoing = outgoing.reshape(groups, capacity, model_width)
        received = lax.all_to_all(outgoing, "expert", split_axis=0, concat_axis=0, tiled=True)
        shape_in = received.shape
        flattened = received.reshape(-1, model_width)

        def compute(rows_in):
            rows_in = rms_normed(rows_in, norm_scale)
            return swiglu(rows_in, gate_matrix, up_matrix, down_matrix)

        def skip_compute(rows_in):
            return jnp.zeros_like(rows_in)

        result = lax.cond(active, compute, skip_compute, flattened)
        computed = result.reshape(shape_in)
        returned = lax.all_to_all(computed, "expert", split_axis=0, concat_axis=0, tiled=True)
        picked = returned.reshape(groups * capacity, model_width)[target].reshape(
            tok_rows, fanout, model_width
        )
        combined = residual.astype(jnp.float32) + jnp.sum(
            weights[:, :, None] * picked.astype(jnp.float32), axis=1
        )
        return combined.astype(jnp.bfloat16)

    def advance(moment, state_pair):
        incoming, stream = state_pair
        micro_idx = moment - position
        active = jnp.logical_and(micro_idx >= 0, micro_idx < micro_count)
        chosen = jnp.clip(micro_idx, 0, micro_count - 1)
        entering = lax.dynamic_index_in_dim(tokens, chosen, 0, keepdims=False)
        residual = jnp.where(position == 0, entering, incoming)
        route_ids = lax.dynamic_index_in_dim(expert_ids[0], chosen, 0, keepdims=False)
        weights = lax.dynamic_index_in_dim(route_weight[0], chosen, 0, keepdims=False)
        stepped = layer_step(residual, route_ids, weights, active)
        result = jnp.where(active, stepped, residual)
        stored = lax.dynamic_update_index_in_dim(stream, result, chosen, 0)
        stream = jnp.where(active, stored, stream)
        incoming = passed_along(result, "section", 1)
        return (incoming, stream)

    starting = (
        jnp.zeros((tok_rows, model_width), jnp.bfloat16),
        jnp.zeros((micro_count, tok_rows, model_width), jnp.bfloat16),
    )
    finished = lax.fori_loop(0, micro_count + sections - 1, advance, starting)
    return finished[1][None]


def solution(mesh):
    return jax.shard_map(
        per_device,
        mesh=mesh,
        in_specs=(
            P(None, "expert", None),
            P("section", None),
            P("section", "expert", None, None),
            P("section", "expert", None, None),
            P("section", "expert", None, None),
            P("section", None, "expert", None),
            P("section", None, "expert", None),
        ),
        out_specs=P("section", None, "expert", None),
        check_vma=False,
    )
```

profile of v0, /device:TPU:1, one launch (start us, length us, event | category | flops | bytes accessed | tf_op | source)
XLA Modules:
  0.0 2193.8 jit_solution(16647509857745943082)
XLA Ops:
  8.7 2185.1 %while.17 = (s32[]{:T(128)}, bf16[128,2048]{1,0:T(8,128)(2,1)S(1)}, bf16[2,128,2048]{2,1,0:T(8,128)(2,1)}, s32[]{:T(128)}, pred[]{:T(512)}, /*index=5*/bf16[2,12...) while((s32[]{:T(128)}, bf16[128,2048]{1,0:T(8,128)(2,1)S(1)}, ...), condition=%wide.region_11.12_spmd, body=%wide.region_0.11_spmd.sunk | while | flops 7370317824 | bytes 142093072 | solution.py:106
  28.6 91.2 %all-to-all-done = bf16[32,25,2048]{2,1,0:T(8,128)(2,1)} async-done(((bf16[32,25,2048]{2,1,0:T(8,128)(2,1)}), bf16[32,25,2048]{2,1,0:T(8,128)(2,1)}, u32[]{:S(2)}, u32[]{:S(2)}) %all-to-all-start) | async-done | bytes 3276832 | tf_op jit(solution)/shard_map/while/body/eval_jaxpr/all_to_all | solution.py:64
  130.9 66.0 %all-to-all-done.1 = bf16[32,25,2048]{2,1,0:T(8,128)(2,1)} async-done(((bf16[32,25,2048]{2,1,0:T(8,128)(2,1)}), bf16[32,25,2048]{2,1,0:T(8,128)(2,1)}, u32[]{:S(2)}, u32[]{:S(2)}) %all-to-all-start.1) | async-done | bytes 3276832 | tf_op jit(solution)/shard_map/while/body/eval_jaxpr/all_to_all | solution.py:77
  218.2 34.7 %collective-permute-start = (bf16[128,2048]{1,0:T(8,128)(2,1)S(1)}, bf16[128,2048]{1,0:T(8,128)(2,1)S(1)}, u32[]{:S(2)}, u32[]{:S(2)}) collective-permute-start(bf16[128,2048]{1,0:T(8,128)(2,1)S(1)} %get-tuple-element.462), channel_id=1, source_target_pairs={{0,32},{32,64},{64,96},{96,128},{128,160},{160,192},{192,224},{1,3... | collective-permute-start | bytes 1572872 | tf_op jit(solution)/shard_map/while/body/eval_jaxpr/ppermute | solution.py:12
  275.9 88.5 %all-to-all-done = bf16[32,25,2048]{2,1,0:T(8,128)(2,1)} async-done(((bf16[32,25,2048]{2,1,0:T(8,128)(2,1)}), bf16[32,25,2048]{2,1,0:T(8,128)(2,1)}, u32[]{:S(2)}, u32[]{:S(2)}) %all-to-all-start) | async-done | bytes 3276832 | tf_op jit(solution)/shard_map/while/body/eval_jaxpr/all_to_all | solution.py:64
  364.4 27.6 %conditional.5 = (bf16[800,2048]{1,0:T(8,128)(2,1)S(1)}) conditional(s32[]{:T(128)} %convert_element_type.102, () %tuple.58, (bf16[32,25,2048]{2,1,0:T(8,128)(2,1)}, f32[1,2048]{1,0:T(1,128)S(1)}, bf16[2048,704]{1,0:T(8,128)(2,1)}, bf16[2048,704]{1,0:T(8,128)(2,1)}, bf16[704,2048]{1,0:T(8,128)(2,1)}) %tuple.61), branch_computations={%region_7.7_spmd, %region_8.9_spmd} | conditional | flops 6940365824 | bytes 54220708 | solution.py:75
  400.1 90.6 %all-to-all-done.1 = bf16[32,25,2048]{2,1,0:T(8,128)(2,1)} async-done(((bf16[32,25,2048]{2,1,0:T(8,128)(2,1)}), bf16[32,25,2048]{2,1,0:T(8,128)(2,1)}, u32[]{:S(2)}, u32[]{:S(2)}) %all-to-all-start.1) | async-done | bytes 3276832 | tf_op jit(solution)/shard_map/while/body/eval_jaxpr/all_to_all | solution.py:77
  536.6 90.6 %all-to-all-done = bf16[32,25,2048]{2,1,0:T(8,128)(2,1)} async-done(((bf16[32,25,2048]{2,1,0:T(8,128)(2,1)}), bf16[32,25,2048]{2,1,0:T(8,128)(2,1)}, u32[]{:S(2)}, u32[]{:S(2)}) %all-to-all-start) | async-done | bytes 3276832 | tf_op jit(solution)/shard_map/while/body/eval_jaxpr/all_to_all | solution.py:64
  627.2 27.6 %conditional.5 = (bf16[800,2048]{1,0:T(8,128)(2,1)S(1)}) conditional(s32[]{:T(128)} %convert_element_type.102, () %tuple.58, (bf16[32,25,2048]{2,1,0:T(8,128)(2,1)}, f32[1,2048]{1,0:T(1,128)S(1)}, bf16[2048,704]{1,0:T(8,128)(2,1)}, bf16[2048,704]{1,0:T(8,128)(2,1)}, bf16[704,2048]{1,0:T(8,128)(2,1)}) %tuple.61), branch_computations={%region_7.7_spmd, %region_8.9_spmd} | conditional | flops 6940365824 | bytes 54220708 | solution.py:75
  663.0 66.2 %all-to-all-done.1 = bf16[32,25,2048]{2,1,0:T(8,128)(2,1)} async-done(((bf16[32,25,2048]{2,1,0:T(8,128)(2,1)}), bf16[32,25,2048]{2,1,0:T(8,128)(2,1)}, u32[]{:S(2)}, u32[]{:S(2)}) %all-to-all-start.1) | async-done | bytes 3276832 | tf_op jit(solution)/shard_map/while/body/eval_jaxpr/all_to_all | solution.py:77
  771.3 91.3 %all-to-all-done = bf16[32,25,2048]{2,1,0:T(8,128)(2,1)} async-done(((bf16[32,25,2048]{2,1,0:T(8,128)(2,1)}), bf16[32,25,2048]{2,1,0:T(8,128)(2,1)}, u32[]{:S(2)}, u32[]{:S(2)}) %all-to-all-start) | async-done | bytes 3276832 | tf_op jit(solution)/shard_map/while/body/eval_jaxpr/all_to_all | solution.py:64
  872.8 92.8 %all-to-all-done.1 = bf16[32,25,2048]{2,1,0:T(8,128)(2,1)} async-done(((bf16[32,25,2048]{2,1,0:T(8,128)(2,1)}), bf16[32,25,2048]{2,1,0:T(8,128)(2,1)}, u32[]{:S(2)}, u32[]{:S(2)}) %all-to-all-start.1) | async-done | bytes 3276832 | tf_op jit(solution)/shard_map/while/body/eval_jaxpr/all_to_all | solution.py:77
  1013.9 89.3 %all-to-all-done = bf16[32,25,2048]{2,1,0:T(8,128)(2,1)} async-done(((bf16[32,25,2048]{2,1,0:T(8,128)(2,1)}), bf16[32,25,2048]{2,1,0:T(8,128)(2,1)}, u32[]{:S(2)}, u32[]{:S(2)}) %all-to-all-start) | async-done | bytes 3276832 | tf_op jit(solution)/shard_map/while/body/eval_jaxpr/all_to_all | solution.py:64
  1111.7 91.0 %all-to-all-done.1 = bf16[32,25,2048]{2,1,0:T(8,128)(2,1)} async-done(((bf16[32,25,2048]{2,1,0:T(8,128)(2,1)}), bf16[32,25,2048]{2,1,0:T(8,128)(2,1)}, u32[]{:S(2)}, u32[]{:S(2)}) %all-to-all-start.1) | async-done | bytes 3276832 | tf_op jit(solution)/shard_map/while/body/eval_jaxpr/all_to_all | solution.py:77
  1246.4 91.3 %all-to-all-done = bf16[32,25,2048]{2,1,0:T(8,128)(2,1)} async-done(((bf16[32,25,2048]{2,1,0:T(8,128)(2,1)}), bf16[32,25,2048]{2,1,0:T(8,128)(2,1)}, u32[]{:S(2)}, u32[]{:S(2)}) %all-to-all-start) | async-done | bytes 3276832 | tf_op jit(solution)/shard_map/while/body/eval_jaxpr/all_to_all | solution.py:64
  1347.9 92.8 %all-to-all-done.1 = bf16[32,25,2048]{2,1,0:T(8,128)(2,1)} async-done(((bf16[32,25,2048]{2,1,0:T(8,128)(2,1)}), bf16[32,25,2048]{2,1,0:T(8,128)(2,1)}, u32[]{:S(2)}, u32[]{:S(2)}) %all-to-all-start.1) | async-done | bytes 3276832 | tf_op jit(solution)/shard_map/while/body/eval_jaxpr/all_to_all | solution.py:77
  1495.5 82.9 %all-to-all-done = bf16[32,25,2048]{2,1,0:T(8,128)(2,1)} async-done(((bf16[32,25,2048]{2,1,0:T(8,128)(2,1)}), bf16[32,25,2048]{2,1,0:T(8,128)(2,1)}, u32[]{:S(2)}, u32[]{:S(2)}) %all-to-all-start) | async-done | bytes 3276832 | tf_op jit(solution)/shard_map/while/body/eval_jaxpr/all_to_all | solution.py:64
  1587.5 86.4 %all-to-all-done.1 = bf16[32,25,2048]{2,1,0:T(8,128)(2,1)} async-done(((bf16[32,25,2048]{2,1,0:T(8,128)(2,1)}), bf16[32,25,2048]{2,1,0:T(8,128)(2,1)}, u32[]{:S(2)}, u32[]{:S(2)}) %all-to-all-start.1) | async-done | bytes 3276832 | tf_op jit(solution)/shard_map/while/body/eval_jaxpr/all_to_all | solution.py:77
  1736.3 76.7 %all-to-all-done = bf16[32,25,2048]{2,1,0:T(8,128)(2,1)} async-done(((bf16[32,25,2048]{2,1,0:T(8,128)(2,1)}), bf16[32,25,2048]{2,1,0:T(8,128)(2,1)}, u32[]{:S(2)}, u32[]{:S(2)}) %all-to-all-start) | async-done | bytes 3276832 | tf_op jit(solution)/shard_map/while/body/eval_jaxpr/all_to_all | solution.py:64
  1821.6 77.1 %all-to-all-done.1 = bf16[32,25,2048]{2,1,0:T(8,128)(2,1)} async-done(((bf16[32,25,2048]{2,1,0:T(8,128)(2,1)}), bf16[32,25,2048]{2,1,0:T(8,128)(2,1)}, u32[]{:S(2)}, u32[]{:S(2)}) %all-to-all-start.1) | async-done | bytes 3276832 | tf_op jit(solution)/shard_map/while/body/eval_jaxpr/all_to_all | solution.py:77
  1919.9 34.0 %collective-permute-start = (bf16[128,2048]{1,0:T(8,128)(2,1)S(1)}, bf16[128,2048]{1,0:T(8,128)(2,1)S(1)}, u32[]{:S(2)}, u32[]{:S(2)}) collective-permute-start(bf16[128,2048]{1,0:T(8,128)(2,1)S(1)} %get-tuple-element.462), channel_id=1, source_target_pairs={{0,32},{32,64},{64,96},{96,128},{128,160},{160,192},{192,224},{1,3... | collective-permute-start | bytes 1572872 | tf_op jit(solution)/shard_map/while/body/eval_jaxpr/ppermute | solution.py:12
  1972.7 78.4 %all-to-all-done = bf16[32,25,2048]{2,1,0:T(8,128)(2,1)} async-done(((bf16[32,25,2048]{2,1,0:T(8,128)(2,1)}), bf16[32,25,2048]{2,1,0:T(8,128)(2,1)}, u32[]{:S(2)}, u32[]{:S(2)}) %all-to-all-start) | async-done | bytes 3276832 | tf_op jit(solution)/shard_map/while/body/eval_jaxpr/all_to_all | solution.py:64
  2062.2 63.7 %all-to-all-done.1 = bf16[32,25,2048]{2,1,0:T(8,128)(2,1)} async-done(((bf16[32,25,2048]{2,1,0:T(8,128)(2,1)}), bf16[32,25,2048]{2,1,0:T(8,128)(2,1)}, u32[]{:S(2)}, u32[]{:S(2)}) %all-to-all-start.1) | async-done | bytes 3276832 | tf_op jit(solution)/shard_map/while/body/eval_jaxpr/all_to_all | solution.py:77
  2147.3 40.4 %collective-permute-start = (bf16[128,2048]{1,0:T(8,128)(2,1)S(1)}, bf16[128,2048]{1,0:T(8,128)(2,1)S(1)}, u32[]{:S(2)}, u32[]{:S(2)}) collective-permute-start(bf16[128,2048]{1,0:T(8,128)(2,1)S(1)} %get-tuple-element.462), channel_id=1, source_target_pairs={{0,32},{32,64},{64,96},{96,128},{128,160},{160,192},{192,224},{1,3... | collective-permute-start | bytes 1572872 | tf_op jit(solution)/shard_map/while/body/eval_jaxpr/ppermute | solution.py:12
  (362 shorter events, 587.0 us)
Async XLA Ops:
  16.6 103.2 %all-to-all-start = ((bf16[32,25,2048]{2,1,0:T(8,128)(2,1)}), bf16[32,25,2048]{2,1,0:T(8,128)(2,1)}, u32[]{:S(2)}, u32[]{:S(2)}) async-start(bf16[32,25,2048]{2,1,0:T(8,128)(2,1)} %reshape.185), calls=%async_computation | async-start | bytes 8388608 | tf_op jit(solution)/shard_map/while/body/eval_jaxpr/all_to_all | solution.py:64
  123.1 73.8 %all-to-all-start.1 = ((bf16[32,25,2048]{2,1,0:T(8,128)(2,1)}), bf16[32,25,2048]{2,1,0:T(8,128)(2,1)}, u32[]{:S(2)}, u32[]{:S(2)}) async-start(bf16[32,25,2048]{2,1,0:T(8,128)(2,1)} %reshape.186), calls=%async_computation.1 | async-start | bytes 8388608 | tf_op jit(solution)/shard_map/while/body/eval_jaxpr/all_to_all | solution.py:77
  218.2 40.8 %collective-permute-start = (bf16[128,2048]{1,0:T(8,128)(2,1)S(1)}, bf16[128,2048]{1,0:T(8,128)(2,1)S(1)}, u32[]{:S(2)}, u32[]{:S(2)}) collective-permute-start(bf16[128,2048]{1,0:T(8,128)(2,1)S(1)} %get-tuple-element.462), channel_id=1, source_target_pairs={{0,32},{32,64},{64,96},{96,128},{128,160},{160,192},{192,224},{1,3... | collective-permute-start | bytes 1572872 | tf_op jit(solution)/shard_map/while/body/eval_jaxpr/ppermute | solution.py:12
  269.0 95.3 %all-to-all-start = ((bf16[32,25,2048]{2,1,0:T(8,128)(2,1)}), bf16[32,25,2048]{2,1,0:T(8,128)(2,1)}, u32[]{:S(2)}, u32[]{:S(2)}) async-start(bf16[32,25,2048]{2,1,0:T(8,128)(2,1)} %reshape.185), calls=%async_computation | async-start | bytes 8388608 | tf_op jit(solution)/shard_map/while/body/eval_jaxpr/all_to_all | solution.py:64
  394.9 95.9 %all-to-all-start.1 = ((bf16[32,25,2048]{2,1,0:T(8,128)(2,1)}), bf16[32,25,2048]{2,1,0:T(8,128)(2,1)}, u32[]{:S(2)}, u32[]{:S(2)}) async-start(bf16[32,25,2048]{2,1,0:T(8,128)(2,1)} %reshape.186), calls=%async_computation.1 | async-start | bytes 8388608 | tf_op jit(solution)/shard_map/while/body/eval_jaxpr/all_to_all | solution.py:77
  530.1 97.1 %all-to-all-start = ((bf16[32,25,2048]{2,1,0:T(8,128)(2,1)}), bf16[32,25,2048]{2,1,0:T(8,128)(2,1)}, u32[]{:S(2)}, u32[]{:S(2)}) async-start(bf16[32,25,2048]{2,1,0:T(8,128)(2,1)} %reshape.185), calls=%async_computation | async-start | bytes 8388608 | tf_op jit(solution)/shard_map/while/body/eval_jaxpr/all_to_all | solution.py:64
  657.7 71.4 %all-to-all-start.1 = ((bf16[32,25,2048]{2,1,0:T(8,128)(2,1)}), bf16[32,25,2048]{2,1,0:T(8,128)(2,1)}, u32[]{:S(2)}, u32[]{:S(2)}) async-start(bf16[32,25,2048]{2,1,0:T(8,128)(2,1)} %reshape.186), calls=%async_computation.1 | async-start | bytes 8388608 | tf_op jit(solution)/shard_map/while/body/eval_jaxpr/all_to_all | solution.py:77
  766.3 96.3 %all-to-all-start = ((bf16[32,25,2048]{2,1,0:T(8,128)(2,1)}), bf16[32,25,2048]{2,1,0:T(8,128)(2,1)}, u32[]{:S(2)}, u32[]{:S(2)}) async-start(bf16[32,25,2048]{2,1,0:T(8,128)(2,1)} %reshape.185), calls=%async_computation | async-start | bytes 8388608 | tf_op jit(solution)/shard_map/while/body/eval_jaxpr/all_to_all | solution.py:64
  865.9 99.6 %all-to-all-start.1 = ((bf16[32,25,2048]{2,1,0:T(8,128)(2,1)}), bf16[32,25,2048]{2,1,0:T(8,128)(2,1)}, u32[]{:S(2)}, u32[]{:S(2)}) async-start(bf16[32,25,2048]{2,1,0:T(8,128)(2,1)} %reshape.186), calls=%async_computation.1 | async-start | bytes 8388608 | tf_op jit(solution)/shard_map/while/body/eval_jaxpr/all_to_all | solution.py:77
  986.9 13.9 collective-permute-start
  1008.6 94.6 %all-to-all-start = ((bf16[32,25,2048]{2,1,0:T(8,128)(2,1)}), bf16[32,25,2048]{2,1,0:T(8,128)(2,1)}, u32[]{:S(2)}, u32[]{:S(2)}) async-start(bf16[32,25,2048]{2,1,0:T(8,128)(2,1)} %reshape.185), calls=%async_computation | async-start | bytes 8388608 | tf_op jit(solution)/shard_map/while/body/eval_jaxpr/all_to_all | solution.py:64
  1106.5 96.2 %all-to-all-start.1 = ((bf16[32,25,2048]{2,1,0:T(8,128)(2,1)}), bf16[32,25,2048]{2,1,0:T(8,128)(2,1)}, u32[]{:S(2)}, u32[]{:S(2)}) async-start(bf16[32,25,2048]{2,1,0:T(8,128)(2,1)} %reshape.186), calls=%async_computation.1 | async-start | bytes 8388608 | tf_op jit(solution)/shard_map/while/body/eval_jaxpr/all_to_all | solution.py:77
  1239.9 97.8 %all-to-all-start = ((bf16[32,25,2048]{2,1,0:T(8,128)(2,1)}), bf16[32,25,2048]{2,1,0:T(8,128)(2,1)}, u32[]{:S(2)}, u32[]{:S(2)}) async-start(bf16[32,25,2048]{2,1,0:T(8,128)(2,1)} %reshape.185), calls=%async_computation | async-start | bytes 8388608 | tf_op jit(solution)/shard_map/while/body/eval_jaxpr/all_to_all | solution.py:64
  1341.0 99.6 %all-to-all-start.1 = ((bf16[32,25,2048]{2,1,0:T(8,128)(2,1)}), bf16[32,25,2048]{2,1,0:T(8,128)(2,1)}, u32[]{:S(2)}, u32[]{:S(2)}) async-start(bf16[32,25,2048]{2,1,0:T(8,128)(2,1)} %reshape.186), calls=%async_computation.1 | async-start | bytes 8388608 | tf_op jit(solution)/shard_map/while/body/eval_jaxpr/all_to_all | solution.py:77
  1462.0 16.6 collective-permute-start
  1486.4 92.0 %all-to-all-start = ((bf16[32,25,2048]{2,1,0:T(8,128)(2,1)}), bf16[32,25,2048]{2,1,0:T(8,128)(2,1)}, u32[]{:S(2)}, u32[]{:S(2)}) async-start(bf16[32,25,2048]{2,1,0:T(8,128)(2,1)} %reshape.185), calls=%async_computation | async-start | bytes 8388608 | tf_op jit(solution)/shard_map/while/body/eval_jaxpr/all_to_all | solution.py:64
  1581.8 92.1 %all-to-all-start.1 = ((bf16[32,25,2048]{2,1,0:T(8,128)(2,1)}), bf16[32,25,2048]{2,1,0:T(8,128)(2,1)}, u32[]{:S(2)}, u32[]{:S(2)}) async-start(bf16[32,25,2048]{2,1,0:T(8,128)(2,1)} %reshape.186), calls=%async_computation.1 | async-start | bytes 8388608 | tf_op jit(solution)/shard_map/while/body/eval_jaxpr/all_to_all | solution.py:77
  1695.2 26.8 %collective-permute-start = (bf16[128,2048]{1,0:T(8,128)(2,1)S(1)}, bf16[128,2048]{1,0:T(8,128)(2,1)S(1)}, u32[]{:S(2)}, u32[]{:S(2)}) collective-permute-start(bf16[128,2048]{1,0:T(8,128)(2,1)S(1)} %get-tuple-element.462), channel_id=1, source_target_pairs={{0,32},{32,64},{64,96},{96,128},{128,160},{160,192},{192,224},{1,3... | collective-permute-start | bytes 1572872 | tf_op jit(solution)/shard_map/while/body/eval_jaxpr/ppermute | solution.py:12
  1729.8 83.2 %all-to-all-start = ((bf16[32,25,2048]{2,1,0:T(8,128)(2,1)}), bf16[32,25,2048]{2,1,0:T(8,128)(2,1)}, u32[]{:S(2)}, u32[]{:S(2)}) async-start(bf16[32,25,2048]{2,1,0:T(8,128)(2,1)} %reshape.185), calls=%async_computation | async-start | bytes 8388608 | tf_op jit(solution)/shard_map/while/body/eval_jaxpr/all_to_all | solution.py:64
  1816.3 82.3 %all-to-all-start.1 = ((bf16[32,25,2048]{2,1,0:T(8,128)(2,1)}), bf16[32,25,2048]{2,1,0:T(8,128)(2,1)}, u32[]{:S(2)}, u32[]{:S(2)}) async-start(bf16[32,25,2048]{2,1,0:T(8,128)(2,1)} %reshape.186), calls=%async_computation.1 | async-start | bytes 8388608 | tf_op jit(solution)/shard_map/while/body/eval_jaxpr/all_to_all | solution.py:77
  1919.9 40.1 %collective-permute-start = (bf16[128,2048]{1,0:T(8,128)(2,1)S(1)}, bf16[128,2048]{1,0:T(8,128)(2,1)S(1)}, u32[]{:S(2)}, u32[]{:S(2)}) collective-permute-start(bf16[128,2048]{1,0:T(8,128)(2,1)S(1)} %get-tuple-element.462), channel_id=1, source_target_pairs={{0,32},{32,64},{64,96},{96,128},{128,160},{160,192},{192,224},{1,3... | collective-permute-start | bytes 1572872 | tf_op jit(solution)/shard_map/while/body/eval_jaxpr/ppermute | solution.py:12
  1967.8 83.3 %all-to-all-start = ((bf16[32,25,2048]{2,1,0:T(8,128)(2,1)}), bf16[32,25,2048]{2,1,0:T(8,128)(2,1)}, u32[]{:S(2)}, u32[]{:S(2)}) async-start(bf16[32,25,2048]{2,1,0:T(8,128)(2,1)} %reshape.185), calls=%async_computation | async-start | bytes 8388608 | tf_op jit(solution)/shard_map/while/body/eval_jaxpr/all_to_all | solution.py:64
  2054.5 71.5 %all-to-all-start.1 = ((bf16[32,25,2048]{2,1,0:T(8,128)(2,1)}), bf16[32,25,2048]{2,1,0:T(8,128)(2,1)}, u32[]{:S(2)}, u32[]{:S(2)}) async-start(bf16[32,25,2048]{2,1,0:T(8,128)(2,1)} %reshape.186), calls=%async_computation.1 | async-start | bytes 8388608 | tf_op jit(solution)/shard_map/while/body/eval_jaxpr/all_to_all | solution.py:77
  2147.3 46.6 %collective-permute-start = (bf16[128,2048]{1,0:T(8,128)(2,1)S(1)}, bf16[128,2048]{1,0:T(8,128)(2,1)S(1)}, u32[]{:S(2)}, u32[]{:S(2)}) collective-permute-start(bf16[128,2048]{1,0:T(8,128)(2,1)S(1)} %get-tuple-element.462), channel_id=1, source_target_pairs={{0,32},{32,64},{64,96},{96,128},{128,160},{160,192},{192,224},{1,3... | collective-permute-start | bytes 1572872 | tf_op jit(solution)/shard_map/while/body/eval_jaxpr/ppermute | solution.py:12
  (36 other events, 382.9 us)
where the time goes:
time: 2200 us; the launch traced here: 2190 us
  waiting for transfers between devices  1560 us (71%)
  starting transfers between devices  269 us (12%)
  local copies, waits for them, and re-layouts  215 us (10%)
  other arithmetic  105 us (5%)
  matrix products  41 us (2%)
    all_to_all x9, waiting for transfers between devices, layer_step(): lax.all_to_all(outgoing, 'expert', split_axis=0, concat_axis=0, tiled=True)  780 us
    all_to_all x9, waiting for transfers between devices, layer_step(): lax.all_to_all(computed, 'expert', split_axis=0, concat_axis=0, tiled=True)  727 us
    ppermute x9, starting transfers between devices, passed_along(): return lax.ppermute(block, axis, route)  154 us
    all_to_all x9, starting transfers between devices, layer_step(): lax.all_to_all(outgoing, 'expert', split_axis=0, concat_axis=0, tiled=True)  62.5 us
    reduce_sum x9, other arithmetic, layer_step(): jnp.sum(weights[:, :, None] * picked.astype(jnp.float32), axis=1)  60.6 us
    convert_element_type x9, local copies, waits for them, and re-layouts, layer_step(): picked.astype(jnp.float32)  58.7 us
    ppermute x9, waiting for transfers between devices, passed_along(): return lax.ppermute(block, axis, route)  54.9 us
    all_to_all x9, starting transfers between devices, layer_step(): lax.all_to_all(computed, 'expert', split_axis=0, concat_axis=0, tiled=True)  52.8 us
  transfers between devices with their start and end apart: 27, of which 27 were waited for; matrix products, arithmetic and copies ran while one was open for 0% of the time, Pallas kernels for 0%

commit v1 on v0

v1 whole, which is shorter than its diff:
```python
import functools

import jax
import jax.numpy as jnp
from jax import lax
from jax.experimental import pallas as pl
from jax.experimental.pallas import tpu as pltpu
from jax.sharding import PartitionSpec as P

EPSILON = 1e-06
X_SIZE = 4
SLOT = 32
LANES = 128
COLS = 512
MESH = pl.DeviceIdType.MESH


def relay_kernel(
    sections,
    ring,
    tokens,
    gain,
    w_gate,
    w_up,
    w_down,
    ids,
    route,
    out,
    ag,
    xs,
    xr,
    ret,
    abuf,
    bbuf,
    hop,
    comb,
    z_send,
    z_recv,
    x_send,
    x_recv,
    r_send,
    r_recv,
    a_send,
    a_recv,
    b_send,
    b_recv,
    h_send,
    h_recv,
):
    micro, rows, width = tokens.shape
    top = ids.shape[-1]
    experts = ring * X_SIZE
    far_a = ring // 2
    far_b = ring // 2 - 1
    tiles = width // COLS
    sec = lax.axis_index("section")
    pos = lax.axis_index("expert")
    z = pos // X_SIZE
    x = pos % X_SIZE
    right = ((z + 1) % ring) * X_SIZE + x
    left = ((z + ring - 1) % ring) * X_SIZE + x

    def x_peer(offset):
        return z * X_SIZE + (x + offset) % X_SIZE

    barrier = pltpu.get_barrier_semaphore()
    for peer in [right, left] + [x_peer(o) for o in range(1, X_SIZE)]:
        pl.semaphore_signal(barrier, inc=1, device_id=(sec, peer), device_id_type=MESH)
    for other in [(sec + 1) % sections, (sec + sections - 1) % sections]:
        pl.semaphore_signal(barrier, inc=1, device_id=(other, pos), device_id_type=MESH)
    pl.semaphore_wait(barrier, X_SIZE + 3)

    def remote(src, dst, send, recv, where):
        return pltpu.make_async_remote_copy(
            src_ref=src,
            dst_ref=dst,
            send_sem=send,
            recv_sem=recv,
            device_id=where,
            device_id_type=MESH,
        )

    def z_copy(m, frm, to, peer):
        return remote(
            ag.at[m, frm], ag.at[m, to], z_send.at[m, to], z_recv.at[m, to], (sec, peer)
        )

    def lump(j, d):
        return pl.ds(pl.multiple_of(j * LANES + d * SLOT, SLOT), SLOT)

    def x_copy(m, j, o):
        return remote(
            xs.at[m, lump(j, (x + o) % X_SIZE)],
            xr.at[m, lump(j, x)],
            x_send.at[m, j, o - 1],
            x_recv.at[m, j, o - 1],
            (sec, x_peer(o)),
        )

    def r_copy(m, j, o):
        return remote(
            xr.at[m, lump(j, (x + o) % X_SIZE)],
            ret.at[m, lump(j, x)],
            r_send.at[m, j, o - 1],
            r_recv.at[m, j, o - 1],
            (sec, x_peer(o)),
        )

    def a_copy(m, r):
        return remote(
            abuf.at[m, r], abuf.at[m, r + 1], a_send.at[m, r], a_recv.at[m, r], (sec, left)
        )

    def b_copy(m, r):
        return remote(
            bbuf.at[m, r], bbuf.at[m, r + 1], b_send.at[m, r], b_recv.at[m, r], (sec, right)
        )

    def h_copy(m, c):
        cols = pl.ds(c * COLS, COLS)
        return remote(
            out.at[m, :, cols],
            hop.at[m, :, cols],
            h_send.at[m, c],
            h_recv.at[m, c],
            ((sec + 1) % sections, pos),
        )

    lane = lax.broadcasted_iota(jnp.int32, (LANES, LANES), 1)
    line = lax.broadcasted_iota(jnp.int32, (LANES, LANES), 0)
    mine = z * X_SIZE + lane // SLOT
    spread_slot = (line == mine).astype(jnp.bfloat16)
    spread_weight = (line == mine + experts).astype(jnp.bfloat16)
    slot_of_lane = (lane % SLOT).astype(jnp.float32)
    earlier = (lane < line).astype(jnp.bfloat16)

    def dot(a, b):
        return jnp.dot(a, b, preferred_element_type=jnp.float32)

    def col_loop(body):
        @pl.loop(0, tiles)
        def _(c):
            body(pl.ds(pl.multiple_of(c * COLS, COLS), COLS))

    def pick_rows(m, j):
        meta = ag[m, j, :, width:]
        hit = dot(meta, spread_slot) == slot_of_lane
        comb[j] = jnp.where(hit, dot(meta, spread_weight), 0.0).astype(jnp.bfloat16)
        pick = jnp.transpose(hit.astype(jnp.float32)).astype(jnp.bfloat16)
        block = pl.ds(pl.multiple_of(j * LANES, LANES), LANES)

        def tile(cols):
            xs[m, block, cols] = dot(pick, ag[m, j, :, cols]).astype(jnp.bfloat16)

        col_loop(tile)
        for o in range(1, X_SIZE):
            x_copy(m, j, o).start()
        xr[m, lump(j, x), :] = xs[m, lump(j, x), :]

    def expert(m, g):
        for j in (2 * g, 2 * g + 1):
            for o in range(1, X_SIZE):
                x_copy(m, j, o).wait_recv()
        group = pl.ds(pl.multiple_of(g * 2 * LANES, 2 * LANES), 2 * LANES)
        gate = dot(xr[m, group, :], w_gate[...])
        up = dot(xr[m, group, :], w_up[...])
        act = (gate / (1.0 + jnp.exp(-gate)) * up).astype(jnp.bfloat16)

        def tile(cols):
            xr[m, group, cols] = dot(act, w_down[:, cols]).astype(jnp.bfloat16)

        col_loop(tile)
        for j in (2 * g, 2 * g + 1):
            for o in range(1, X_SIZE):
                r_copy(m, j, o).start()
            ret[m, lump(j, x), :] = xr[m, lump(j, x), :]

    def returned(m, j):
        for o in range(1, X_SIZE):
            r_copy(m, j, o).wait_recv()

    def combined(m, j, cols):
        block = pl.ds(pl.multiple_of(j * LANES, LANES), LANES)
        return dot(comb[j], ret[m, block, cols])

    @pl.when(sec == 0)
    def _():
        @pl.loop(0, micro * rows // 16)
        def _(i):
            m = i // (rows // 16)
            r = pl.ds(pl.multiple_of((i % (rows // 16)) * 16, 16), 16)
            hop[m, r, :] = tokens[m, r, :]

    @pl.loop(0, micro)
    def _(m):
        @pl.when(sec > 0)
        def _():
            for c in range(tiles):
                h_copy(m, c).wait_recv()

        @pl.loop(0, rows // 16)
        def _(i):
            r = pl.ds(pl.multiple_of(i * 16, 16), 16)
            value = hop[m, r, :].astype(jnp.float32)
            inverse = lax.rsqrt(jnp.mean(value * value, axis=-1, keepdims=True) + EPSILON)
            ag[m, 0, r, :width] = (value * inverse * gain[...]).astype(jnp.bfloat16)

        member = jnp.zeros((rows, LANES), jnp.float32)
        weight = jnp.zeros((rows, LANES), jnp.float32)
        for k in range(top):
            choice = ids[m, :, k : k + 1]
            member = member + (choice == lane).astype(jnp.float32)
            weight = weight + jnp.where(choice + experts == lane, route[m, :, k : k + 1], 0.0)
        before = dot(earlier, member.astype(jnp.bfloat16))
        slot = jnp.where(member > 0.0, before, -1.0)
        ag[m, 0, :, width:] = jnp.where(lane < experts, slot, weight).astype(jnp.bfloat16)

        z_copy(m, 0, 1, right).start()
        z_copy(m, 0, 2, left).start()
        pick_rows(m, 0)

        @pl.loop(1, far_a + 2)
        def _(k):
            @pl.when(k <= far_a)
            def _():
                near = 2 * k - 1
                z_copy(m, near, near, right).wait_recv()

                @pl.when(k < far_a)
                def _():
                    z_copy(m, near, near + 2, right).start()

                @pl.when(k <= far_b)
                def _():
                    z_copy(m, near + 1, near + 1, left).wait_recv()

                    @pl.when(k < far_b)
                    def _():
                        z_copy(m, near + 1, near + 3, left).start()

                pick_rows(m, near)

                @pl.when(k <= far_b)
                def _():
                    pick_rows(m, near + 1)

            @pl.when(k >= 2)
            def _():
                expert(m, k - 2)

        @pl.loop(0, far_a)
        def _(r):
            ja = 2 * (far_a - r) - 1
            returned(m, ja)

            @pl.when(r == 0)
            def _():
                def tile(cols):
                    abuf[m, r, :, cols] = combined(m, ja, cols).astype(jnp.bfloat16)

                col_loop(tile)

            @pl.when(r > 0)
            def _():
                a_copy(m, r - 1).wait_recv()

                def tile(cols):
                    abuf[m, r, :, cols] = (
                        abuf[m, r, :, cols].astype(jnp.float32) + combined(m, ja, cols)
                    ).astype(jnp.bfloat16)

                col_loop(tile)

            a_copy(m, r).start()

            @pl.when(r < far_b)
            def _():
                jb = 2 * (far_b - r)
                returned(m, jb)

                @pl.when(r == 0)
                def _():
                    def tile(cols):
                        bbuf[m, r, :, cols] = combined(m, jb, cols).astype(jnp.bfloat16)

                    col_loop(tile)

                @pl.when(r > 0)
                def _():
                    b_copy(m, r - 1).wait_recv()

                    def tile(cols):
                        bbuf[m, r, :, cols] = (
                            bbuf[m, r, :, cols].astype(jnp.float32) + combined(m, jb, cols)
                        ).astype(jnp.bfloat16)

                    col_loop(tile)

                b_copy(m, r).start()

        returned(m, 0)
        b_copy(m, far_b - 1).wait_recv()
        a_copy(m, far_a - 1).wait_recv()
        for c in range(tiles):
            cols = pl.ds(c * COLS, COLS)
            total = (
                combined(m, 0, cols)
                + abuf[m, far_a, :, cols].astype(jnp.float32)
                + bbuf[m, far_b, :, cols].astype(jnp.float32)
            )
            out[m, :, cols] = (hop[m, :, cols].astype(jnp.float32) + total).astype(jnp.bfloat16)

            @pl.when(sec < sections - 1)
            def _():
                h_copy(m, c).start()

    @pl.loop(0, micro)
    def _(m):
        for j in range(1, ring):
            z_copy(m, j, j, right).wait_send()
        for j in range(ring):
            for o in range(1, X_SIZE):
                x_copy(m, j, o).wait_send()
                r_copy(m, j, o).wait_send()
        for r in range(far_a):
            a_copy(m, r).wait_send()
        for r in range(far_b):
            b_copy(m, r).wait_send()

        @pl.when(sec < sections - 1)
        def _():
            for c in range(tiles):
                h_copy(m, c).wait_send()


def per_device(tokens, norm_gain, w_gate, w_up, w_down, expert_ids, route_weight):
    sections = lax.axis_size("section")
    ring = lax.axis_size("expert") // X_SIZE
    micro, rows, width = tokens.shape
    block = (micro, ring * LANES, width)
    dma = pltpu.SemaphoreType.DMA
    result = pl.pallas_call(
        functools.partial(relay_kernel, sections, ring),
        out_shape=jax.ShapeDtypeStruct((micro, rows, width), jnp.bfloat16),
        in_specs=[pl.BlockSpec(memory_space=pltpu.VMEM)] * 7,
        out_specs=pl.BlockSpec(memory_space=pltpu.VMEM),
        scratch_shapes=[
            pltpu.VMEM((micro, ring, rows, width + LANES), jnp.bfloat16),
            pltpu.VMEM(block, jnp.bfloat16),
            pltpu.VMEM(block, jnp.bfloat16),
            pltpu.VMEM(block, jnp.bfloat16),
            pltpu.VMEM((micro, ring // 2 + 1, rows, width), jnp.bfloat16),
            pltpu.VMEM((micro, ring // 2, rows, width), jnp.bfloat16),
            pltpu.VMEM((micro, rows, width), jnp.bfloat16),
            pltpu.VMEM((ring, rows, LANES), jnp.bfloat16),
            dma((micro, ring)),
            dma((micro, ring)),
            dma((micro, ring, X_SIZE - 1)),
            dma((micro, ring, X_SIZE - 1)),
            dma((micro, ring, X_SIZE - 1)),
            dma((micro, ring, X_SIZE - 1)),
            dma((micro, ring // 2)),
            dma((micro, ring // 2)),
            dma((micro, ring // 2)),
            dma((micro, ring // 2)),
            dma((micro, width // COLS)),
            dma((micro, width // COLS)),
        ],
        compiler_params=pltpu.CompilerParams(
            collective_id=0, has_side_effects=True, vmem_limit_bytes=67_000_000
        ),
        name="relay",
    )(
        tokens,
        norm_gain,
        w_gate[0, 0],
        w_up[0, 0],
        w_down[0, 0],
        expert_ids[0],
        route_weight[0],
    )
    return result[None]


def solution(mesh):
    return jax.shard_map(
        per_device,
        mesh=mesh,
        in_specs=(
            P(None, "expert", None),
            P("section", None),
            P("section", "expert", None, None),
            P("section", "expert", None, None),
            P("section", "expert", None, None),
            P("section", None, "expert", None),
            P("section", None, "expert", None),
        ),
        out_specs=P("section", None, "expert", None),
        check_vma=False,
    )
```

time: 2200 us -> 1160 us (0.53)
  the two profiles are of different devices: /device:TPU:1 before, /device:TPU:57 now
where the time goes in v1:
time: 1160 us
  Pallas kernels  1150 us (99%)
  local copies, waits for them, and re-layouts  12.9 us (1%)
    pallas_call x1, Pallas kernels, per_device(): pl.pallas_call(functools.partial(relay_kernel, sections, ring), out_shape...  1150 us

profile of v1, /device:TPU:57, one launch (start us, length us, event | category | flops | bytes accessed | tf_op | source)
XLA Modules:
  0.0 1162.8 jit_solution(5560761581748965912)
XLA Ops:
  0.0 1.5 copy.10
  1.5 1.5 copy.11
  3.0 0.0 copy-start
  3.0 4.7 copy.8
  7.7 0.0 copy-done
  7.7 2.8 copy.9
  10.6 1149.9 %relay.1 = bf16[2,128,2048]{2,1,0:T(8,128)(2,1)} custom-call(bf16[2,128,2048]{2,1,0:T(8,128)(2,1)} %tokens.1, f32[1,2048]{1,0:T(1,128)} %gain.1, bf16[2048,704]{1,0:T(8,128)(2,1)} %bitcast.6, bf16[2048,704]{1,0:T(8,128)(2,1)} %bitcast.7, bf16[704,2048]{1,0:T(8,128)(2,1)} %bitcast.9, s32[2,128,6]{2,1,0:T(8,128)} %bitcast.10, f32[2,128,6]{2,1,0:T(8,128)} %bitcast.11), custom_call_target="tpu_custom_call" | custom-call | tf_op jit(solution)/shard_map/relay/pallas_call | solution.py:342
  1160.5 2.3 copy.13
Async XLA Ops:
  3.0 4.8 copy-start

commit v2 on v0

v2 whole, which is shorter than its diff:
```python
import functools

import jax
import jax.numpy as jnp
from jax import lax
from jax.experimental import pallas as pl
from jax.experimental.pallas import tpu as pltpu
from jax.sharding import PartitionSpec as P

EPSILON = 1e-06
X_SIZE = 4
Y_SIZE = 4
CORES = 2
RING = 8
SLOT = 32
LANES = 128
COLS = 512
PIECES = 4
MESH = pl.DeviceIdType.MESH
LAG = 2
START_GROUPS = PIECES + LAG
FAR_A = RING // 2
FAR_B = RING // 2 - 1


def relay_kernel(
    tokens,
    gains,
    w_gate,
    w_up,
    w_down,
    ids,
    route,
    out,
    f_gate,
    f_up,
    f_down,
    v_gate,
    v_up,
    v_down,
    local_meta,
    meta,
    ag,
    xs,
    xr,
    ret,
    comb,
    part,
    abuf,
    bbuf,
    obuf,
    y_send,
    y_recv,
    d_send,
    d_recv,
    m_send,
    m_recv,
    t_send,
    t_recv,
    z_send,
    z_recv,
    x_send,
    x_recv,
    r_send,
    r_recv,
    a_send,
    a_recv,
    b_send,
    b_recv,
    o_send,
    o_recv,
    v_sem,
):
    micro, rows, width = tokens.shape
    own = rows // Y_SIZE
    top = ids.shape[-1]
    experts = RING * X_SIZE
    layers = Y_SIZE * CORES
    lumps = 2 * SLOT
    every = RING * own
    tiles = width // COLS
    sec = lax.axis_index("section")
    pos = lax.axis_index("expert")
    y = sec // CORES
    c = sec % CORES
    z = pos // X_SIZE
    x = pos % X_SIZE
    half = z // Y_SIZE
    quarter = z % Y_SIZE

    def at(zz):
        return ((zz + 2 * RING) % RING) * X_SIZE + x

    right = at(z + 1)
    left = at(z - 1)
    sibling = y * CORES + 1 - c
    y_peer = [((y + 1) % Y_SIZE) * CORES + c, ((y + Y_SIZE - 1) % Y_SIZE) * CORES + c]

    def remote(src, dst, send, recv, where):
        return pltpu.make_async_remote_copy(
            src_ref=src,
            dst_ref=dst,
            send_sem=send,
            recv_sem=recv,
            device_id=where,
            device_id_type=MESH,
        )

    def dot(a, b):
        return jnp.dot(a, b, preferred_element_type=jnp.float32)

    def dot_t(a, b):
        return lax.dot_general(
            a, b, (((1,), (1,)), ((), ())), preferred_element_type=jnp.float32
        )

    def col_loop(body):
        @pl.loop(0, tiles)
        def _(i):
            body(pl.ds(pl.multiple_of(i * COLS, COLS), COLS))

    given = (w_gate, w_up, w_down)
    full = (f_gate, f_up, f_down)
    step = (
        w_gate.shape[0] // (2 * PIECES),
        w_up.shape[0] // (2 * PIECES),
        w_down.shape[0] // (2 * PIECES),
    )

    def part_rows(t, i, d):
        return pl.ds(pl.multiple_of((d * PIECES + i) * step[t], step[t]), step[t])

    def y_copy(src, q, i, d, t):
        r = part_rows(t, i, d)
        return remote(
            src.at[r],
            full[t].at[2 * q + c, r],
            y_send.at[q, i, d, t],
            y_recv.at[q, i, d, t],
            (y_peer[d], pos),
        )

    def d_copy(src, q, i, d, t):
        r = part_rows(t, i, d)
        return remote(
            src.at[r],
            full[t].at[2 * q + c, r],
            d_send.at[q, i, d, t],
            d_recv.at[q, i, d, t],
            (sibling, pos),
        )

    def away_from(q, d):
        return (y - q + Y_SIZE) % Y_SIZE if d == 0 else (q - y + Y_SIZE) % Y_SIZE

    def stream(group, s):
        for k in range(Y_SIZE):
            t = (s - LAG * k) % 3
            g = group + (s - LAG * k) // 3
            valid = jnp.logical_and(g >= 0, g < Y_SIZE * PIECES)
            g = jnp.maximum(g, 0)
            q = g // PIECES
            i = g % PIECES
            for d in range(2):

                @pl.when(jnp.logical_and(valid, away_from(q, d) == k))
                def _():
                    held = given[t] if k == 0 else full[t].at[2 * q + c]
                    if k > 0:
                        y_copy(held, q, i, d, t).wait_recv()
                    if k < Y_SIZE - 1:
                        y_copy(held, q, i, d, t).start()
                    d_copy(held, q, i, d, t).start()

    def stream_done(q, i):
        for d in range(2):
            away = away_from(q, d)
            for t in range(3):
                held = full[t].at[2 * q + c]

                @pl.when(away < Y_SIZE - 1)
                def _():
                    y_copy(held, q, i, d, t).wait_send()

                d_copy(held, q, i, d, t).wait_send()

    def v_copy(src, dst, t):
        return pltpu.make_async_copy(src, dst, v_sem.at[t])

    held_v = (v_gate, v_up, v_down)

    def load_weights(layer):
        q = layer // 2

        @pl.when(layer % 2 != c)
        def _():
            for i in range(PIECES):
                for d in range(2):
                    for t in range(3):
                        r = part_rows(t, i, d)
                        remote(
                            full[t].at[layer, r],
                            full[t].at[layer, r],
                            d_send.at[q, i, d, t],
                            d_recv.at[q, i, d, t],
                            (sibling, pos),
                        ).wait_recv()

        @pl.when(layer == sec)
        def _():
            for t in range(3):
                v_copy(given[t], held_v[t], t).start()

        @pl.when(layer != sec)
        def _():
            for t in range(3):
                v_copy(full[t].at[layer], held_v[t], t).start()

    def weights_ready(layer):
        for t in range(3):
            v_copy(full[t].at[layer], held_v[t], t).wait()

    lane = lax.broadcasted_iota(jnp.int32, (rows, LANES), 1)
    line = lax.broadcasted_iota(jnp.int32, (rows, LANES), 0)
    earlier = (lane < line).astype(jnp.bfloat16)

    def m_copy(m, zz):
        return remote(
            local_meta.at[m],
            meta.at[sec, half],
            m_send.at[m, zz],
            m_recv.at[sec, half],
            (quarter * CORES + m, at(zz)),
        )

    def m_is_self(m, zz):
        return jnp.logical_and(quarter * CORES + m == sec, zz == z)

    for m in range(micro):
        member = jnp.zeros((rows, LANES), jnp.float32)
        weight = jnp.zeros((rows, LANES), jnp.float32)
        for k in range(top):
            choice = ids[m, :, k : k + 1]
            member = member + (choice == lane).astype(jnp.float32)
            weight = weight + jnp.where(choice + experts == lane, route[m, :, k : k + 1], 0.0)
        before = dot(earlier, member.astype(jnp.bfloat16))
        slot = jnp.where(member > 0.0, before, -1.0)
        local_meta[m] = jnp.where(lane < experts, slot, weight).astype(jnp.bfloat16)

    def t_copy(i):
        return remote(
            tokens.at[c, pl.ds(i * own, own)],
            obuf.at[1],
            t_send.at[i],
            t_recv,
            (sec, at(half * Y_SIZE + i)),
        )

    for i in range(Y_SIZE):

        @pl.when(jnp.logical_and(quarter == y, quarter != i))
        def _():
            t_copy(i).start()

        @pl.when(jnp.logical_and(quarter == y, quarter == i))
        def _():
            obuf[1] = tokens[c, pl.ds(i * own, own), :]

    for m in range(micro):
        for zz in range(RING):

            @pl.when(jnp.logical_not(m_is_self(m, zz)))
            def _():
                m_copy(m, zz).start()

            @pl.when(m_is_self(m, zz))
            def _():
                meta[sec, half] = local_meta[m]

    @pl.loop(0, START_GROUPS)
    def _(g):
        for s in range(3):
            stream(g, s)

    @pl.when(quarter != y)
    def _():
        t_copy(0).wait_recv()

    wide = 4 * lumps
    w_lane = lax.broadcasted_iota(jnp.int32, (LANES, wide), 1)
    w_line = lax.broadcasted_iota(jnp.int32, (LANES, wide), 0)
    target = z * X_SIZE + w_lane // lumps
    spread_slot = (w_line == target).astype(jnp.bfloat16)
    spread_weight = (w_line == target + experts).astype(jnp.bfloat16)
    g_lane = lax.broadcasted_iota(jnp.int32, (rows, wide), 1)
    slot_of_lane = (g_lane % SLOT).astype(jnp.float32)
    block_of_lane = (g_lane // SLOT) % 2

    def rows_of(zz):
        return pl.ds(pl.multiple_of(((zz + 2 * RING) % RING) * own, own), own)

    def z_copy(p, k, d, src):
        return remote(
            ag.at[p, rows_of(src)],
            ag.at[p, rows_of(src)],
            z_send.at[p, d, k],
            z_recv.at[p, d, k],
            (sec, (right, left)[d]),
        )

    def lump(d):
        return pl.ds(pl.multiple_of(d * lumps, lumps), lumps)

    def x_copy(p, o):
        return remote(
            xs.at[p, lump((x + o) % X_SIZE)],
            xr.at[p, lump(x)],
            x_send.at[p, o - 1],
            x_recv.at[p, o - 1],
            (sec, z * X_SIZE + (x + o) % X_SIZE),
        )

    def r_copy(p, o):
        return remote(
            xr.at[p, lump((x + o) % X_SIZE)],
            ret.at[p, lump(x)],
            r_send.at[p, o - 1],
            r_recv.at[p, o - 1],
            (sec, z * X_SIZE + (x + o) % X_SIZE),
        )

    def a_copy(p, r):
        return remote(
            abuf.at[p, r], abuf.at[p, r + 1], a_send.at[p, r], a_recv.at[p, r], (sec, left)
        )

    def b_copy(p, r):
        return remote(
            bbuf.at[p, r], bbuf.at[p, r + 1], b_send.at[p, r], b_recv.at[p, r], (sec, right)
        )

    home = half * Y_SIZE + y

    def o_copy(p, layer):
        return remote(
            obuf.at[p],
            out.at[c, pl.ds(pl.multiple_of(quarter * own, own), own)],
            o_send.at[p],
            o_recv.at[c, quarter],
            (layer, at(home)),
        )

    def o_is_self(layer):
        return jnp.logical_and(layer == sec, home == z)

    def sends_done(p, layer):
        for k in range(1, FAR_A + 1):
            z_copy(p, k, 0, z).wait_send()
        for k in range(1, FAR_B + 1):
            z_copy(p, k, 1, z).wait_send()
        for o in range(1, X_SIZE):
            x_copy(p, o).wait_send()
            r_copy(p, o).wait_send()
        for r in range(FAR_A):
            a_copy(p, r).wait_send()
        for r in range(FAR_B):
            b_copy(p, r).wait_send()

        @pl.when(jnp.logical_not(o_is_self(layer)))
        def _():
            o_copy(p, layer).wait_send()

    def streams(layer, lo, hi):
        @pl.when(layer < layers - 2)
        def _():
            for s in range(lo, hi):
                stream(START_GROUPS + 2 * layer + s // 3, s % 3)

    @pl.loop(0, layers)
    def _(layer):
        p = layer % 2

        value = obuf[1 - p].astype(jnp.float32)
        inverse = lax.rsqrt(jnp.mean(value * value, axis=-1, keepdims=True) + EPSILON)
        gain = gains[pl.ds(layer, 1), :]
        ag[p, rows_of(z), :] = (value * inverse * gain).astype(jnp.bfloat16)
        z_copy(p, 1, 0, z).start()
        z_copy(p, 1, 1, z).start()
        load_weights(layer)
        streams(layer, 0, 2)
        for h in range(2):

            @pl.when(jnp.logical_not(jnp.logical_and(layer == sec, home - half * Y_SIZE + h * Y_SIZE == z)))
            def _():
                remote(
                    meta.at[layer, h],
                    meta.at[layer, h],
                    m_send.at[0, 0],
                    m_recv.at[layer, h],
                    (sec, right),
                ).wait_recv()

        for k in range(1, FAR_A + 1):
            z_copy(p, k, 0, z - k).wait_recv()
            if k < FAR_A:
                z_copy(p, k + 1, 0, z - k).start()
            if k <= FAR_B:
                z_copy(p, k, 1, z + k).wait_recv()
                if k < FAR_B:
                    z_copy(p, k + 1, 1, z + k).start()

        @pl.when(layer >= 1)
        def _():
            sends_done(1 - p, layer - 1)

        for h in range(2):
            table = meta[layer, h]
            hit = jnp.logical_and(dot(table, spread_slot) == slot_of_lane, block_of_lane == h)
            scaled = jnp.where(hit, dot(table, spread_weight), 0.0)
            comb[0, pl.ds(h * rows, rows), :] = hit.astype(jnp.float32).astype(jnp.bfloat16)
            comb[1, pl.ds(h * rows, rows), :] = scaled.astype(jnp.bfloat16)
        pick = jnp.transpose(comb[0].astype(jnp.float32)).astype(jnp.bfloat16)

        def pick_tile(cols):
            xs[p, :, cols] = dot(pick, ag[p, :, cols]).astype(jnp.bfloat16)

        col_loop(pick_tile)
        for o in range(1, X_SIZE):
            x_copy(p, o).start()
        xr[p, lump(x), :] = xs[p, lump(x), :]
        streams(layer, 2, 4)
        weights_ready(layer)
        for o in range(1, X_SIZE):
            x_copy(p, o).wait_recv()

        gate = dot_t(xr[p], v_gate[...])
        up = dot_t(xr[p], v_up[...])
        act = (gate / (1.0 + jnp.exp(-gate)) * up).astype(jnp.bfloat16)

        def down_tile(cols):
            xr[p, :, cols] = dot(act, v_down[:, cols]).astype(jnp.bfloat16)

        col_loop(down_tile)
        for o in range(1, X_SIZE):
            r_copy(p, o).start()
        ret[p, lump(x), :] = xr[p, lump(x), :]
        streams(layer, 4, 6)
        for o in range(1, X_SIZE):
            r_copy(p, o).wait_recv()

        def comb_tile(cols):
            part[:, cols] = dot(comb[1], ret[p, :, cols])

        col_loop(comb_tile)

        for r in range(FAR_A):
            mine = part[rows_of(z - FAR_A + r), :]
            if r > 0:
                a_copy(p, r - 1).wait_recv()
                mine = mine + abuf[p, r].astype(jnp.float32)
            abuf[p, r] = mine.astype(jnp.bfloat16)
            a_copy(p, r).start()
            if r < FAR_B:
                mine = part[rows_of(z + FAR_B - r), :]
                if r > 0:
                    b_copy(p, r - 1).wait_recv()
                    mine = mine + bbuf[p, r].astype(jnp.float32)
                bbuf[p, r] = mine.astype(jnp.bfloat16)
                b_copy(p, r).start()
        b_copy(p, FAR_B - 1).wait_recv()
        a_copy(p, FAR_A - 1).wait_recv()
        total = (
            part[rows_of(z), :]
            + abuf[p, FAR_A].astype(jnp.float32)
            + bbuf[p, FAR_B].astype(jnp.float32)
        )
        obuf[p] = (obuf[1 - p].astype(jnp.float32) + total).astype(jnp.bfloat16)

        @pl.when(jnp.logical_not(o_is_self(layer)))
        def _():
            o_copy(p, layer).start()

        @pl.when(o_is_self(layer))
        def _():
            out[c, pl.ds(pl.multiple_of(quarter * own, own), own), :] = obuf[p]

    sends_done(1, layers - 1)

    @pl.loop(0, Y_SIZE)
    def _(q):
        @pl.loop(0, PIECES)
        def _(i):
            stream_done(q, i)

    for i in range(Y_SIZE):

        @pl.when(jnp.logical_and(quarter == y, quarter != i))
        def _():
            t_copy(i).wait_send()

    for m in range(micro):
        for zz in range(RING):

            @pl.when(jnp.logical_not(m_is_self(m, zz)))
            def _():
                m_copy(m, zz).wait_send()

    for m in range(micro):
        for i in range(Y_SIZE):

            @pl.when(jnp.logical_not(jnp.logical_and(quarter * CORES + m == sec, i == quarter)))
            def _():
                r = pl.ds(i * own, own)
                remote(
                    out.at[m, r],
                    out.at[m, r],
                    o_send.at[0],
                    o_recv.at[m, i],
                    (sec, right),
                ).wait_recv()


def per_device(tokens, norm_gain, w_gate, w_up, w_down, expert_ids, route_weight):
    micro, rows, width = tokens.shape
    layers = Y_SIZE * CORES
    own = rows // Y_SIZE
    every = RING * own
    lined = 2 * SLOT * X_SIZE
    hidden = w_gate.shape[-1]
    gains = lax.all_gather(norm_gain, "section", axis=0, tiled=True)
    dma = pltpu.SemaphoreType.DMA
    vmem = pl.BlockSpec(memory_space=pltpu.VMEM)
    hbm = pl.BlockSpec(memory_space=pl.ANY)
    bf16 = jnp.bfloat16
    result = pl.pallas_call(
        relay_kernel,
        out_shape=(
            jax.ShapeDtypeStruct((micro, rows, width), bf16),
            jax.ShapeDtypeStruct((layers, hidden, width), bf16),
            jax.ShapeDtypeStruct((layers, hidden, width), bf16),
            jax.ShapeDtypeStruct((layers, hidden, width), bf16),
        ),
        in_specs=[vmem, vmem, hbm, hbm, hbm, vmem, vmem],
        out_specs=(vmem, hbm, hbm, hbm),
        scratch_shapes=[
            pltpu.VMEM((hidden, width), bf16),
            pltpu.VMEM((hidden, width), bf16),
            pltpu.VMEM((hidden, width), bf16),
            pltpu.VMEM((micro, rows, LANES), bf16),
            pltpu.VMEM((layers, 2, rows, LANES), bf16),
            pltpu.VMEM((2, every, width), bf16),
            pltpu.VMEM((2, lined, width), bf16),
            pltpu.VMEM((2, lined, width), bf16),
            pltpu.VMEM((2, lined, width), bf16),
            pltpu.VMEM((2, every, lined), bf16),
            pltpu.VMEM((every, width), jnp.float32),
            pltpu.VMEM((2, FAR_A + 1, own, width), bf16),
            pltpu.VMEM((2, FAR_B + 1, own, width), bf16),
            pltpu.VMEM((2, own, width), bf16),
            dma((Y_SIZE, PIECES, 2, 3)),
            dma((Y_SIZE, PIECES, 2, 3)),
            dma((Y_SIZE, PIECES, 2, 3)),
            dma((Y_SIZE, PIECES, 2, 3)),
            dma((micro, RING)),
            dma((layers, 2)),
            dma((Y_SIZE,)),
            dma,
            dma((2, 2, FAR_A + 1)),
            dma((2, 2, FAR_A + 1)),
            dma((2, X_SIZE - 1)),
            dma((2, X_SIZE - 1)),
            dma((2, X_SIZE - 1)),
            dma((2, X_SIZE - 1)),
            dma((2, FAR_A)),
            dma((2, FAR_A)),
            dma((2, FAR_B)),
            dma((2, FAR_B)),
            dma((2,)),
            dma((micro, Y_SIZE)),
            dma((3,)),
        ],
        compiler_params=pltpu.CompilerParams(
            has_side_effects=True, vmem_limit_bytes=56_000_000
        ),
        name="relay",
    )(
        tokens,
        gains,
        w_gate[0, 0].T,
        w_up[0, 0].T,
        w_down[0, 0],
        expert_ids[0],
        route_weight[0],
    )
    return result[0][None]


def solution(mesh):
    return jax.shard_map(
        per_device,
        mesh=mesh,
        in_specs=(
            P(None, "expert", None),
            P("section", None),
            P("section", "expert", None, None),
            P("section", "expert", None, None),
            P("section", "expert", None, None),
            P("section", None, "expert", None),
            P("section", None, "expert", None),
        ),
        out_specs=P("section", None, "expert", None),
        check_vma=False,
    )
```

time: 2200 us -> 711 us (0.32)
  the two profiles are of different devices: /device:TPU:1 before, /device:TPU:57 now
where the time goes in v2:
time: 711 us
  Pallas kernels  694 us (98%)
  blocking collectives  13.5 us (2%)
    pallas_call x1, Pallas kernels, per_device(): pl.pallas_call(relay_kernel, out_shape=(jax.ShapeDtypeStruct((micro, rows...  694 us

profile of v2, /device:TPU:57, one launch (start us, length us, event | category | flops | bytes accessed | tf_op | source)
XLA Modules:
  0.0 711.0 jit_solution(14320492848213352723)
XLA Ops:
  0.0 13.5 %all-gather = f32[8,1,2048]{2,1,0:T(1,128)S(1)} all-gather(f32[1,1,2048]{2,1,0:T(1,128)} %bitcast.21), channel_id=1, replica_groups=mesh['section'=8,'expert'=32] {'section'}, dimensions={0}, use_global_device_ids=true | all-gather | bytes 73728 | tf_op jit(solution)/shard_map/all_gather | solution.py:530
  13.5 0.8 copy.10
  14.3 0.8 copy.11
  15.2 693.5 %relay.1 = (bf16[2,128,2048]{2,1,0:T(8,128)(2,1)}, bf16[8,704,2048]{2,1,0:T(8,128)(2,1)}, bf16[8,704,2048]{2,1,0:T(8,128)(2,1)}, bf16[8,704,2048]{2,1,0:T(8,128)(2,1)}) custom-call(bf16[2,128,2048]{2,1,0:T(8,128)(2,1)} %tokens.1, f32[8,2048]{1,0:T(8,128)S(1)} %bitcast.16, bf16[704,2048]{1,0:T(8,128)(2,1)} %bitcast.17, bf16[704,2048]{1,0:T(8,128)(2,1)} %bitcast.18, ...), custom_call_target="tpu_custom_call" | custom-call | tf_op jit(solution)/shard_map/relay/pallas_call | solution.py:535
  708.7 2.3 copy.16
  (1 shorter events, 0.0 us)

commit v3 on v2

--- a/solution.py
+++ b/solution.py
@@ -17,7 +17,8 @@
 COLS = 512
 PIECES = 4
 MESH = pl.DeviceIdType.MESH
-LAG = 2
+LAG = 3
+STRIPS = 2
 START_GROUPS = PIECES + LAG
 FAR_A = RING // 2
 FAR_B = RING // 2 - 1
@@ -94,7 +95,7 @@
     right = at(z + 1)
     left = at(z - 1)
     sibling = y * CORES + 1 - c
-    y_peer = [((y + 1) % Y_SIZE) * CORES + c, ((y + Y_SIZE - 1) % Y_SIZE) * CORES + c]
+    y_peer = (jnp.where(c == 0, y + 1, y + Y_SIZE - 1) % Y_SIZE) * CORES + c
 
     def remote(src, dst, send, recv, where):
         return pltpu.make_async_remote_copy(
@@ -114,8 +115,8 @@
             a, b, (((1,), (1,)), ((), ())), preferred_element_type=jnp.float32
         )
 
-    def col_loop(body):
-        @pl.loop(0, tiles)
+    def col_loop(body, w):
+        @pl.loop(w * (tiles // STRIPS), (w + 1) * (tiles // STRIPS))
         def _(i):
             body(pl.ds(pl.multiple_of(i * COLS, COLS), COLS))
 
@@ -130,59 +131,74 @@
     def part_rows(t, i, d):
         return pl.ds(pl.multiple_of((d * PIECES + i) * step[t], step[t]), step[t])
 
-    def y_copy(src, q, i, d, t):
+    def y_copy(src, l, i, t):
+        r = part_rows(t, i, c)
+        return remote(
+            src.at[r], full[t].at[l, r], y_send.at[l, i, t], y_recv.at[l, i, t], (y_peer, pos)
+        )
+
+    def d_copy(src, l, i, d, t):
         r = part_rows(t, i, d)
         return remote(
             src.at[r],
-            full[t].at[2 * q + c, r],
-            y_send.at[q, i, d, t],
-            y_recv.at[q, i, d, t],
-            (y_peer[d], pos),
-        )
-
-    def d_copy(src, q, i, d, t):
-        r = part_rows(t, i, d)
-        return remote(
-            src.at[r],
-            full[t].at[2 * q + c, r],
-            d_send.at[q, i, d, t],
-            d_recv.at[q, i, d, t],
+            full[t].at[l, r],
+            d_send.at[l, i, d, t],
+            d_recv.at[l, i, d, t],
             (sibling, pos),
         )
 
-    def away_from(q, d):
-        return (y - q + Y_SIZE) % Y_SIZE if d == 0 else (q - y + Y_SIZE) % Y_SIZE
-
-    def stream(group, s):
+    def away_from(l):
+        q = l // CORES
+        return jnp.where(c == 0, y - q + Y_SIZE, q - y + Y_SIZE) % Y_SIZE
+
+    def stream(group, turn):
         for k in range(Y_SIZE):
-            t = (s - LAG * k) % 3
-            g = group + (s - LAG * k) // 3
-            valid = jnp.logical_and(g >= 0, g < Y_SIZE * PIECES)
+            t = (turn - LAG * k) % 3
+            g = group + (turn - LAG * k) // 3
+            valid = jnp.logical_and(g >= 0, g < layers * PIECES)
             g = jnp.maximum(g, 0)
-            q = g // PIECES
+            l = g // PIECES
             i = g % PIECES
-            for d in range(2):
-
-                @pl.when(jnp.logical_and(valid, away_from(q, d) == k))
+            here = jnp.logical_and(valid, away_from(l) == k)
+            held = full[t].at[l]
+            if k == 0:
+
+                @pl.when(jnp.logical_and(here, l == sec))
                 def _():
-                    held = given[t] if k == 0 else full[t].at[2 * q + c]
-                    if k > 0:
-                        y_copy(held, q, i, d, t).wait_recv()
+                    y_copy(given[t], l, i, t).start()
+                    d_copy(given[t], l, i, 1 - c, t).start()
+                    d_copy(given[t], l, i, c, t).start()
+
+                @pl.when(jnp.logical_and(here, l != sec))
+                def _():
+                    d_copy(held, l, i, c, t).wait_recv()
+                    y_copy(held, l, i, t).start()
+
+            else:
+
+                @pl.when(here)
+                def _():
+                    y_copy(held, l, i, t).wait_recv()
                     if k < Y_SIZE - 1:
-                        y_copy(held, q, i, d, t).start()
-                    d_copy(held, q, i, d, t).start()
-
-    def stream_done(q, i):
-        for d in range(2):
-            away = away_from(q, d)
-            for t in range(3):
-                held = full[t].at[2 * q + c]
-
-                @pl.when(away < Y_SIZE - 1)
-                def _():
-                    y_copy(held, q, i, d, t).wait_send()
-
-                d_copy(held, q, i, d, t).wait_send()
+                        y_copy(held, l, i, t).start()
+                    d_copy(held, l, i, c, t).start()
+
+    def stream_done(l, i):
+        away = away_from(l)
+        for t in range(3):
+            held = full[t].at[l]
+
+            @pl.when(away < Y_SIZE - 1)
+            def _():
+                y_copy(held, l, i, t).wait_send()
+
+            @pl.when(jnp.logical_or(away > 0, l == sec))
+            def _():
+                d_copy(held, l, i, c, t).wait_send()
+
+            @pl.when(l == sec)
+            def _():
+                d_copy(held, l, i, 1 - c, t).wait_send()
 
     def v_copy(src, dst, t):
         return pltpu.make_async_copy(src, dst, v_sem.at[t])
@@ -190,21 +206,11 @@
     held_v = (v_gate, v_up, v_down)
 
     def load_weights(layer):
-        q = layer // 2
-
-        @pl.when(layer % 2 != c)
+        @pl.when(layer != sec)
         def _():
             for i in range(PIECES):
-                for d in range(2):
-                    for t in range(3):
-                        r = part_rows(t, i, d)
-                        remote(
-                            full[t].at[layer, r],
-                            full[t].at[layer, r],
-                            d_send.at[q, i, d, t],
-                            d_recv.at[q, i, d, t],
-                            (sibling, pos),
-                        ).wait_recv()
+                for t in range(3):
+                    d_copy(full[t].at[layer], layer, i, 1 - c, t).wait_recv()
 
         @pl.when(layer == sec)
         def _():
@@ -279,8 +285,8 @@
 
     @pl.loop(0, START_GROUPS)
     def _(g):
-        for s in range(3):
-            stream(g, s)
+        for turn in range(3):
+            stream(g, turn)
 
     @pl.when(quarter != y)
     def _():
@@ -299,44 +305,55 @@
     def rows_of(zz):
         return pl.ds(pl.multiple_of(((zz + 2 * RING) % RING) * own, own), own)
 
-    def z_copy(p, k, d, src):
-        return remote(
-            ag.at[p, rows_of(src)],
-            ag.at[p, rows_of(src)],
-            z_send.at[p, d, k],
-            z_recv.at[p, d, k],
+    def strip(w):
+        return pl.ds(w * (width // STRIPS), width // STRIPS)
+
+    def z_copy(p, k, d, src, w):
+        return remote(
+            ag.at[p, rows_of(src), strip(w)],
+            ag.at[p, rows_of(src), strip(w)],
+            z_send.at[p, d, k, w],
+            z_recv.at[p, d, k, w],
             (sec, (right, left)[d]),
         )
 
     def lump(d):
         return pl.ds(pl.multiple_of(d * lumps, lumps), lumps)
 
-    def x_copy(p, o):
-        return remote(
-            xs.at[p, lump((x + o) % X_SIZE)],
-            xr.at[p, lump(x)],
-            x_send.at[p, o - 1],
-            x_recv.at[p, o - 1],
+    def x_copy(p, o, w):
+        return remote(
+            xs.at[p, lump((x + o) % X_SIZE), strip(w)],
+            xr.at[p, lump(x), strip(w)],
+            x_send.at[p, o - 1, w],
+            x_recv.at[p, o - 1, w],
             (sec, z * X_SIZE + (x + o) % X_SIZE),
         )
 
-    def r_copy(p, o):
-        return remote(
-            xr.at[p, lump((x + o) % X_SIZE)],
-            ret.at[p, lump(x)],
-            r_send.at[p, o - 1],
-            r_recv.at[p, o - 1],
+    def r_copy(p, o, w):
+        return remote(
+            xr.at[p, lump((x + o) % X_SIZE), strip(w)],
+            ret.at[p, lump(x), strip(w)],
+            r_send.at[p, o - 1, w],
+            r_recv.at[p, o - 1, w],
             (sec, z * X_SIZE + (x + o) % X_SIZE),
         )
 
-    def a_copy(p, r):
-        return remote(
-            abuf.at[p, r], abuf.at[p, r + 1], a_send.at[p, r], a_recv.at[p, r], (sec, left)
-        )
-
-    def b_copy(p, r):
-        return remote(
-            bbuf.at[p, r], bbuf.at[p, r + 1], b_send.at[p, r], b_recv.at[p, r], (sec, right)
+    def a_copy(p, r, w):
+        return remote(
+            abuf.at[p, r, :, strip(w)],
+            abuf.at[p, r + 1, :, strip(w)],
+            a_send.at[p, r, w],
+            a_recv.at[p, r, w],
+            (sec, left),
+        )
+
+    def b_copy(p, r, w):
+        return remote(
+            bbuf.at[p, r, :, strip(w)],
+            bbuf.at[p, r + 1, :, strip(w)],
+            b_send.at[p, r, w],
+            b_recv.at[p, r, w],
+            (sec, right),
         )
 
     home = half * Y_SIZE + y
@@ -354,27 +371,32 @@
         return jnp.logical_and(layer == sec, home == z)
 
     def sends_done(p, layer):
-        for k in range(1, FAR_A + 1):
-            z_copy(p, k, 0, z).wait_send()
-        for k in range(1, FAR_B + 1):
-            z_copy(p, k, 1, z).wait_send()
-        for o in range(1, X_SIZE):
-            x_copy(p, o).wait_send()
-            r_copy(p, o).wait_send()
-        for r in range(FAR_A):
-            a_copy(p, r).wait_send()
-        for r in range(FAR_B):
-            b_copy(p, r).wait_send()
+        for w in range(STRIPS):
+            for k in range(1, FAR_A + 1):
+                z_copy(p, k, 0, z, w).wait_send()
+            for k in range(1, FAR_B + 1):
+                z_copy(p, k, 1, z, w).wait_send()
+            for o in range(1, X_SIZE):
+                x_copy(p, o, w).wait_send()
+                r_copy(p, o, w).wait_send()
+            for r in range(FAR_A):
+                a_copy(p, r, w).wait_send()
+            for r in range(FAR_B):
+                b_copy(p, r, w).wait_send()
 
         @pl.when(jnp.logical_not(o_is_self(layer)))
         def _():
             o_copy(p, layer).wait_send()
 
-    def streams(layer, lo, hi):
-        @pl.when(layer < layers - 2)
-        def _():
-            for s in range(lo, hi):
-                stream(START_GROUPS + 2 * layer + s // 3, s % 3)
+    def groups_at(layer, at_point):
+        count = START_GROUPS + PIECES * layer + at_point
+        return jnp.minimum(count, layers * PIECES + LAG)
+
+    def streams(layer, at_point):
+        @pl.loop(groups_at(layer, at_point), groups_at(layer, at_point + 1))
+        def _(g):
+            for turn in range(3):
+                stream(g, turn)
 
     @pl.loop(0, layers)
     def _(layer):
@@ -384,10 +406,11 @@
         inverse = lax.rsqrt(jnp.mean(value * value, axis=-1, keepdims=True) + EPSILON)
         gain = gains[pl.ds(layer, 1), :]
         ag[p, rows_of(z), :] = (value * inverse * gain).astype(jnp.bfloat16)
-        z_copy(p, 1, 0, z).start()
-        z_copy(p, 1, 1, z).start()
+        for w in range(STRIPS):
+            z_copy(p, 1, 0, z, w).start()
+            z_copy(p, 1, 1, z, w).start()
         load_weights(layer)
-        streams(layer, 0, 2)
+        streams(layer, 0)
         for h in range(2):
 
             @pl.when(jnp.logical_not(jnp.logical_and(layer == sec, home - half * Y_SIZE + h * Y_SIZE == z)))
@@ -400,14 +423,15 @@
                     (sec, right),
                 ).wait_recv()
 
-        for k in range(1, FAR_A + 1):
-            z_copy(p, k, 0, z - k).wait_recv()
-            if k < FAR_A:
-                z_copy(p, k + 1, 0, z - k).start()
-            if k <= FAR_B:
-                z_copy(p, k, 1, z + k).wait_recv()
+        for k in range(1, FAR_A):
+            for w in range(STRIPS):
+                z_copy(p, k, 0, z - k, w).wait_recv()
+                z_copy(p, k + 1, 0, z - k, w).start()
+                z_copy(p, k, 1, z + k, w).wait_recv()
                 if k < FAR_B:
-                    z_copy(p, k + 1, 1, z + k).start()
+                    z_copy(p, k + 1, 1, z + k, w).start()
+            if k == 2:
+                streams(layer, 1)
 
         @pl.when(layer >= 1)
         def _():
@@ -421,60 +445,71 @@
             comb[1, pl.ds(h * rows, rows), :] = scaled.astype(jnp.bfloat16)
         pick = jnp.transpose(comb[0].astype(jnp.float32)).astype(jnp.bfloat16)
 
-        def pick_tile(cols):
-            xs[p, :, cols] = dot(pick, ag[p, :, cols]).astype(jnp.bfloat16)
-
-        col_loop(pick_tile)
-        for o in range(1, X_SIZE):
-            x_copy(p, o).start()
-        xr[p, lump(x), :] = xs[p, lump(x), :]
-        streams(layer, 2, 4)
+        for w in range(STRIPS):
+            z_copy(p, FAR_A, 0, z - FAR_A, w).wait_recv()
+
+            def pick_tile(cols):
+                xs[p, :, cols] = dot(pick, ag[p, :, cols]).astype(jnp.bfloat16)
+
+            col_loop(pick_tile, w)
+            for o in range(1, X_SIZE):
+                x_copy(p, o, w).start()
+            xr[p, lump(x), strip(w)] = xs[p, lump(x), strip(w)]
+        streams(layer, 2)
         weights_ready(layer)
-        for o in range(1, X_SIZE):
-            x_copy(p, o).wait_recv()
-
-        gate = dot_t(xr[p], v_gate[...])
-        up = dot_t(xr[p], v_up[...])
+        gate = 0.0
+        up = 0.0
+        for w in range(STRIPS):
+            for o in range(1, X_SIZE):
+                x_copy(p, o, w).wait_recv()
+            gate = gate + dot_t(xr[p, :, strip(w)], v_gate[:, strip(w)])
+            up = up + dot_t(xr[p, :, strip(w)], v_up[:, strip(w)])
         act = (gate / (1.0 + jnp.exp(-gate)) * up).astype(jnp.bfloat16)
-
-        def down_tile(cols):
-            xr[p, :, cols] = dot(act, v_down[:, cols]).astype(jnp.bfloat16)
-
-        col_loop(down_tile)
-        for o in range(1, X_SIZE):
-            r_copy(p, o).start()
-        ret[p, lump(x), :] = xr[p, lump(x), :]
-        streams(layer, 4, 6)
-        for o in range(1, X_SIZE):
-            r_copy(p, o).wait_recv()
-
-        def comb_tile(cols):
-            part[:, cols] = dot(comb[1], ret[p, :, cols])
-
-        col_loop(comb_tile)
+        for w in range(STRIPS):
+
+            def down_tile(cols):
+                xr[p, :, cols] = dot(act, v_down[:, cols]).astype(jnp.bfloat16)
+
+            col_loop(down_tile, w)
+            for o in range(1, X_SIZE):
+                r_copy(p, o, w).start()
+            ret[p, lump(x), strip(w)] = xr[p, lump(x), strip(w)]
+        streams(layer, 3)
 
         for r in range(FAR_A):
-            mine = part[rows_of(z - FAR_A + r), :]
-            if r > 0:
-                a_copy(p, r - 1).wait_recv()
-                mine = mine + abuf[p, r].astype(jnp.float32)
-            abuf[p, r] = mine.astype(jnp.bfloat16)
-            a_copy(p, r).start()
-            if r < FAR_B:
-                mine = part[rows_of(z + FAR_B - r), :]
+            for w in range(STRIPS):
+                if r == 0:
+                    for o in range(1, X_SIZE):
+                        r_copy(p, o, w).wait_recv()
+
+                    def comb_tile(cols):
+                        part[:, cols] = dot(comb[1], ret[p, :, cols])
+
+                    col_loop(comb_tile, w)
+                mine = part[rows_of(z - FAR_A + r), strip(w)]
                 if r > 0:
-                    b_copy(p, r - 1).wait_recv()
-                    mine = mine + bbuf[p, r].astype(jnp.float32)
-                bbuf[p, r] = mine.astype(jnp.bfloat16)
-                b_copy(p, r).start()
-        b_copy(p, FAR_B - 1).wait_recv()
-        a_copy(p, FAR_A - 1).wait_recv()
-        total = (
-            part[rows_of(z), :]
-            + abuf[p, FAR_A].astype(jnp.float32)
-            + bbuf[p, FAR_B].astype(jnp.float32)
-        )
-        obuf[p] = (obuf[1 - p].astype(jnp.float32) + total).astype(jnp.bfloat16)
+                    a_copy(p, r - 1, w).wait_recv()
+                    mine = mine + abuf[p, r, :, strip(w)].astype(jnp.float32)
+                abuf[p, r, :, strip(w)] = mine.astype(jnp.bfloat16)
+                a_copy(p, r, w).start()
+                if r < FAR_B:
+                    mine = part[rows_of(z + FAR_B - r), strip(w)]
+                    if r > 0:
+                        b_copy(p, r - 1, w).wait_recv()
+                        mine = mine + bbuf[p, r, :, strip(w)].astype(jnp.float32)
+                    bbuf[p, r, :, strip(w)] = mine.astype(jnp.bfloat16)
+                    b_copy(p, r, w).start()
+        for w in range(STRIPS):
+            b_copy(p, FAR_B - 1, w).wait_recv()
+            a_copy(p, FAR_A - 1, w).wait_recv()
+            total = (
+                part[rows_of(z), strip(w)]
+                + abuf[p, FAR_A, :, strip(w)].astype(jnp.float32)
+                + bbuf[p, FAR_B, :, strip(w)].astype(jnp.float32)
+            )
+            obuf[p, :, strip(w)] = (
+                obuf[1 - p, :, strip(w)].astype(jnp.float32) + total
+            ).astype(jnp.bfloat16)
 
         @pl.when(jnp.logical_not(o_is_self(layer)))
         def _():
@@ -486,11 +521,11 @@
 
     sends_done(1, layers - 1)
 
-    @pl.loop(0, Y_SIZE)
-    def _(q):
+    @pl.loop(0, layers)
+    def _(l):
         @pl.loop(0, PIECES)
         def _(i):
-            stream_done(q, i)
+            stream_done(l, i)
 
     for i in range(Y_SIZE):
 
@@ -557,24 +592,24 @@
             pltpu.VMEM((2, FAR_A + 1, own, width), bf16),
             pltpu.VMEM((2, FAR_B + 1, own, width), bf16),
             pltpu.VMEM((2, own, width), bf16),
-            dma((Y_SIZE, PIECES, 2, 3)),
-            dma((Y_SIZE, PIECES, 2, 3)),
-            dma((Y_SIZE, PIECES, 2, 3)),
-            dma((Y_SIZE, PIECES, 2, 3)),
+            dma((layers, PIECES, 3)),
+            dma((layers, PIECES, 3)),
+            dma((layers, PIECES, 2, 3)),
+            dma((layers, PIECES, 2, 3)),
             dma((micro, RING)),
             dma((layers, 2)),
             dma((Y_SIZE,)),
             dma,
-            dma((2, 2, FAR_A + 1)),
-            dma((2, 2, FAR_A + 1)),
-            dma((2, X_SIZE - 1)),
-            dma((2, X_SIZE - 1)),
-            dma((2, X_SIZE - 1)),
-            dma((2, X_SIZE - 1)),
-            dma((2, FAR_A)),
-            dma((2, FAR_A)),
-            dma((2, FAR_B)),
-            dma((2, FAR_B)),
+            dma((2, 2, FAR_A + 1, STRIPS)),
+            dma((2, 2, FAR_A + 1, STRIPS)),
+            dma((2, X_SIZE - 1, STRIPS)),
+            dma((2, X_SIZE - 1, STRIPS)),
+            dma((2, X_SIZE - 1, STRIPS)),
+            dma((2, X_SIZE - 1, STRIPS)),
+            dma((2, FAR_A, STRIPS)),
+            dma((2, FAR_A, STRIPS)),
+            dma((2, FAR_B, STRIPS)),
+            dma((2, FAR_B, STRIPS)),
             dma((2,)),
             dma((micro, Y_SIZE)),
             dma((3,)),

time: 711 us -> 635 us (0.89)
  Pallas kernels: 694 us -> 617 us
    pallas_call x1, Pallas kernels: 694 us -> 617 us  [per_device(): pl.pallas_call(relay_kernel, out_shape=(jax.ShapeDtypeStruct((micro, rows...]
where the time goes in v3:
time: 635 us
  Pallas kernels  617 us (97%)
  blocking collectives  13.5 us (2%)
    pallas_call x1, Pallas kernels, per_device(): pl.pallas_call(relay_kernel, out_shape=(jax.ShapeDtypeStruct((micro, rows...  617 us
    all_gather x1, blocking collectives, per_device(): gains = lax.all_gather(norm_gain, 'section', axis=0, tiled=True)  13.5 us

profile of v3, /device:TPU:57, one launch (start us, length us, event | category | flops | bytes accessed | tf_op | source)
XLA Modules:
  0.0 634.9 jit_solution(10782522164106660370)
XLA Ops:
  0.0 13.5 %all-gather = f32[8,1,2048]{2,1,0:T(1,128)S(1)} all-gather(f32[1,1,2048]{2,1,0:T(1,128)} %bitcast.21), channel_id=1, replica_groups=mesh['section'=8,'expert'=32] {'section'}, dimensions={0}, use_global_device_ids=true | all-gather | bytes 73728 | tf_op jit(solution)/shard_map/all_gather | solution.py:565
  13.5 0.8 copy.10
  14.3 0.8 copy.11
  15.2 617.5 %relay.1 = (bf16[2,128,2048]{2,1,0:T(8,128)(2,1)}, bf16[8,704,2048]{2,1,0:T(8,128)(2,1)}, bf16[8,704,2048]{2,1,0:T(8,128)(2,1)}, bf16[8,704,2048]{2,1,0:T(8,128)(2,1)}) custom-call(bf16[2,128,2048]{2,1,0:T(8,128)(2,1)} %tokens.1, f32[8,2048]{1,0:T(8,128)S(1)} %bitcast.16, bf16[704,2048]{1,0:T(8,128)(2,1)} %bitcast.17, bf16[704,2048]{1,0:T(8,128)(2,1)} %bitcast.18, ...), custom_call_target="tpu_custom_call" | custom-call | tf_op jit(solution)/shard_map/relay/pallas_call | solution.py:570
  632.6 2.3 copy.16
  (1 shorter events, 0.0 us)

commit v4 on v3

--- a/solution.py
+++ b/solution.py
@@ -18,7 +18,7 @@
 PIECES = 4
 MESH = pl.DeviceIdType.MESH
 LAG = 3
-STRIPS = 2
+STRIPS = 4
 START_GROUPS = PIECES + LAG
 FAR_A = RING // 2
 FAR_B = RING // 2 - 1
@@ -26,7 +26,7 @@
 
 def relay_kernel(
     tokens,
-    gains,
+    own_gain,
     w_gate,
     w_up,
     w_down,
@@ -50,6 +50,9 @@
     abuf,
     bbuf,
     obuf,
+    gains,
+    g_send,
+    g_recv,
     y_send,
     y_recv,
     d_send,
@@ -253,6 +256,13 @@
         slot = jnp.where(member > 0.0, before, -1.0)
         local_meta[m] = jnp.where(lane < experts, slot, weight).astype(jnp.bfloat16)
 
+    def g_copy(other):
+        return remote(
+            own_gain, gains.at[sec], g_send.at[other], g_recv.at[sec], (other, pos)
+        )
+
+    gains[sec] = own_gain[...]
+
     def t_copy(i):
         return remote(
             tokens.at[c, pl.ds(i * own, own)],
@@ -282,6 +292,12 @@
             @pl.when(m_is_self(m, zz))
             def _():
                 meta[sec, half] = local_meta[m]
+
+    for other in range(layers):
+
+        @pl.when(sec != other)
+        def _():
+            g_copy(other).start()
 
     @pl.loop(0, START_GROUPS)
     def _(g):
@@ -404,7 +420,14 @@
 
         value = obuf[1 - p].astype(jnp.float32)
         inverse = lax.rsqrt(jnp.mean(value * value, axis=-1, keepdims=True) + EPSILON)
-        gain = gains[pl.ds(layer, 1), :]
+
+        @pl.when(layer != sec)
+        def _():
+            remote(
+                gains.at[layer], gains.at[layer], g_send.at[0], g_recv.at[layer], (sec, right)
+            ).wait_recv()
+
+        gain = gains[layer]
         ag[p, rows_of(z), :] = (value * inverse * gain).astype(jnp.bfloat16)
         for w in range(STRIPS):
             z_copy(p, 1, 0, z, w).start()
@@ -519,6 +542,12 @@
         def _():
             out[c, pl.ds(pl.multiple_of(quarter * own, own), own), :] = obuf[p]
 
+    for other in range(layers):
+
+        @pl.when(sec != other)
+        def _():
+            g_copy(other).wait_send()
+
     sends_done(1, layers - 1)
 
     @pl.loop(0, layers)
@@ -562,7 +591,6 @@
     every = RING * own
     lined = 2 * SLOT * X_SIZE
     hidden = w_gate.shape[-1]
-    gains = lax.all_gather(norm_gain, "section", axis=0, tiled=True)
     dma = pltpu.SemaphoreType.DMA
     vmem = pl.BlockSpec(memory_space=pltpu.VMEM)
     hbm = pl.BlockSpec(memory_space=pl.ANY)
@@ -592,6 +620,9 @@
             pltpu.VMEM((2, FAR_A + 1, own, width), bf16),
             pltpu.VMEM((2, FAR_B + 1, own, width), bf16),
             pltpu.VMEM((2, own, width), bf16),
+            pltpu.VMEM((layers, 1, width), jnp.float32),
+            dma((layers,)),
+            dma((layers,)),
             dma((layers, PIECES, 3)),
             dma((layers, PIECES, 3)),
             dma((layers, PIECES, 2, 3)),
@@ -620,7 +651,7 @@
         name="relay",
     )(
         tokens,
-        gains,
+        norm_gain,
         w_gate[0, 0].T,
         w_up[0, 0].T,
         w_down[0, 0],

time: 635 us -> 612 us (0.964)
  blocking collectives: 13.5 us -> 0 us
  Pallas kernels: 617 us -> 607 us
    all_gather x1 -> x0, blocking collectives: 13.5 us -> none  [per_device(): gains = lax.all_gather(norm_gain, 'section', axis=0, tiled=True)]
    pallas_call x1, Pallas kernels: 617 us -> 607 us  [per_device(): pl.pallas_call(relay_kernel, out_shape=(jax.ShapeDtypeStruct((micro, rows...]
where the time goes in v4:
time: 612 us
  Pallas kernels  607 us (99%)
    pallas_call x1, Pallas kernels, per_device(): pl.pallas_call(relay_kernel, out_shape=(jax.ShapeDtypeStruct((micro, rows...  607 us

profile of v4, /device:TPU:57, one launch (start us, length us, event | category | flops | bytes accessed | tf_op | source)
XLA Modules:
  0.0 612.0 jit_solution(15013656954093296964)
XLA Ops:
  0.0 0.8 copy.8
  0.8 0.8 copy.9
  1.7 0.0 copy-start
  1.7 0.7 copy-done
  2.4 607.3 %relay.1 = (bf16[2,128,2048]{2,1,0:T(8,128)(2,1)}, bf16[8,704,2048]{2,1,0:T(8,128)(2,1)}, bf16[8,704,2048]{2,1,0:T(8,128)(2,1)}, bf16[8,704,2048]{2,1,0:T(8,128)(2,1)}) custom-call(bf16[2,128,2048]{2,1,0:T(8,128)(2,1)} %tokens.1, f32[1,2048]{1,0:T(1,128)S(1)} %copy-done, bf16[704,2048]{1,0:T(8,128)(2,1)} %bitcast.12, bf16[704,2048]{1,0:T(8,128)(2,1)} %bitcast.13, ...), custom_call_target="tpu_custom_call" | custom-call | tf_op jit(solution)/shard_map/relay/pallas_call | solution.py:598
  609.7 2.3 copy.11
Async XLA Ops:
  1.7 0.7 copy-start
